TPU v7x, 128 devices: a whole 4x4x4 slice. The times are simulated.
128 devices in a mesh: lat: 8 (over z, core), lon: 16 (over y, x).
Axes of the slice: x: 4, y: 4, z: 4, core: 2. Of those that a mesh axis runs over, the one named last changes fastest.
Arguments:
- increments: bfloat16 [262144, 3, 128], P(('lat', 'lon')), may hold values from -6 to 6
- cotangent: bfloat16 [262144, 128], P(('lat', 'lon')), may hold values from -6 to 6
- owner_perm: int32 [128, 2048], P(('lat', 'lon')), may hold values from 0 to 2047, each once within a row
- coarse_index: int32 [2, 131072], P(None, ('lat', 'lon')), may hold values from 0 to 2047
- coarse_weight: float32 [131072], P(('lat', 'lon')), may hold values from 0.2 to 0.8
- back_index: int32 [2, 262144], P(None, ('lat', 'lon')), may hold values from 0 to 1023
- back_weight: float32 [262144], P(('lat', 'lon')), may hold values from 0.2 to 0.8
- lw_scale: float32 [16, 131072], P(None, ('lat', 'lon')), may hold values from 0.1 to 1
- sw_scale: float32 [14, 131072], P(None, ('lat', 'lon')), may hold values from 0.2 to 2
- sunlit: int32 [131072], P(('lat', 'lon')), may hold values from 0 to 1, as said below
- lw_table: bfloat16 [16, 3, 128, 128], P(None, None, 'lon'), may hold values from -0.3125 to 0.3125
- sw_table: bfloat16 [14, 3, 128, 128], P(None, None, 'lon'), may hold values from -0.3125 to 0.3125
Outputs:
- tendency: bfloat16 [262144, 128], P(('lat', 'lon'))
- gradient: bfloat16 [262144, 3, 128], P(('lat', 'lon'))
Inputs may be any that keep to these rules, and one draw needn't show every extreme that they name: In each device's block of 1024 radiation columns at most 640 are sunlit, and some device has exactly 640.
All inputs are finite; a program needn't handle non-finite values.
Results may differ from a plain program's by a relative error of at most 0.014.
Values may be sent and summed in bfloat16 or wider, within the bound.
No kernel may reach another device: no remote copies, remote signals or barrier semaphores. Data moves between devices by JAX's collectives and lax.ppermute only.
A program may use at most 64 MiB of HBM per device.

v0:
```python
import jax
import jax.numpy as jnp
from jax import lax
from jax.experimental import pallas as pl
from jax.experimental.pallas import tpu as pltpu
from jax.sharding import PartitionSpec as P


ALL = ("lat", "lon")
F32 = jnp.float32
BF16 = jnp.bfloat16
MIB = 1 << 20


def call(kernel, out, flops, limit, scratch=(), specs=None, out_specs=None):
    extra = {} if specs is None else {"in_specs": specs}
    if out_specs is not None:
        extra["out_specs"] = out_specs
    return pl.pallas_call(
        kernel,
        out_shape=out,
        **extra,
        scratch_shapes=scratch,
        compiler_params=pltpu.CompilerParams(vmem_limit_bytes=limit * MIB),
        cost_estimate=pl.CostEstimate(flops=flops, bytes_accessed=4 * MIB, transcendentals=0),
    )


PICK_BLOCKS = (256, 512, 1024, 256)


def starts(blocks):
    return [sum(blocks[:k]) for k in range(len(blocks))]


def pick_kernel(perm_hbm, planes_hbm, last_hbm, out_hbm, perm_ref, data_ref, hot_ref, out_ref, in_sems, out_sems):
    total = perm_ref.shape[1]
    planes = planes_hbm.shape[0]
    first = pltpu.make_async_copy(perm_hbm, perm_ref, in_sems.at[planes + 1])
    first.start()
    loads = [pltpu.make_async_copy(planes_hbm.at[v], data_ref.at[v], in_sems.at[v]) for v in range(planes)]
    loads.append(pltpu.make_async_copy(last_hbm, data_ref.at[planes], in_sems.at[planes]))
    for load in loads:
        load.start()
    first.wait()

    def fill(k):
        start, rows = starts(PICK_BLOCKS)[k], PICK_BLOCKS[k]
        index = jnp.transpose(jnp.broadcast_to(perm_ref[:, start : start + rows], (128, rows)))
        lanes = lax.broadcasted_iota(jnp.int32, (rows, total), 1)
        hot = jnp.concatenate([index] * (total // 128), axis=1) == lanes
        hot_ref[k % 2, :rows, :] = hot.astype(F32).astype(BF16)

    fill(0)
    for load in loads:
        load.wait()
    stores = []
    for k, (start, rows) in enumerate(zip(starts(PICK_BLOCKS), PICK_BLOCKS)):
        data = jnp.concatenate([data_ref[v] for v in range(planes + 1)], axis=1)
        got = jnp.dot(hot_ref[k % 2, :rows, :], data, preferred_element_type=F32)
        out_ref[start : start + rows, :] = got.astype(BF16)
        stores.append(
            pltpu.make_async_copy(
                out_ref.at[pl.ds(start, rows), :], out_hbm.at[pl.ds(start, rows), :], out_sems.at[k]
            )
        )
        stores[-1].start()
        if k + 1 < len(PICK_BLOCKS):
            fill(k + 1)
    for store in stores:
        store.wait()


def pick(perm, planes, last):
    total = perm.shape[1]
    count = planes.shape[0] + 1
    out = jax.ShapeDtypeStruct((total, count * 128), BF16)
    far = pl.BlockSpec(memory_space=pl.ANY)
    scratch = [
        pltpu.VMEM(perm.shape, jnp.int32),
        pltpu.VMEM((count, total, 128), BF16),
        pltpu.VMEM((2, max(PICK_BLOCKS), total), BF16),
        pltpu.VMEM((total, count * 128), BF16),
        pltpu.SemaphoreType.DMA((count + 1,)),
        pltpu.SemaphoreType.DMA((len(PICK_BLOCKS),)),
    ]
    flops = 2 * total * total * count * 128
    return call(pick_kernel, out, flops, 60, scratch, [far] * 3, far)(perm, planes, last)


RESTORE_BLOCKS = (256, 1024, 512, 256)


def restore_kernel(perm_ref, data_ref, planes_hbm, last_hbm, hot_ref, out_ref, sems):
    total = perm_ref.shape[1]
    planes = planes_hbm.shape[0]

    def fill(k):
        start, rows = starts(RESTORE_BLOCKS)[k], RESTORE_BLOCKS[k]
        targets = lax.broadcasted_iota(jnp.int32, (rows, total), 0) + start
        hot = jnp.broadcast_to(perm_ref[...], (rows, total)) == targets
        hot_ref[k % 2, :rows, :] = hot.astype(F32).astype(BF16)

    fill(0)
    stores = []
    for k, (start, rows) in enumerate(zip(starts(RESTORE_BLOCKS), RESTORE_BLOCKS)):
        got = jnp.dot(hot_ref[k % 2, :rows, :], data_ref[...], preferred_element_type=F32).astype(BF16)
        for v in range(planes + 1):
            out_ref[v, start : start + rows, :] = got[:, v * 128 : (v + 1) * 128]
        span = pl.ds(start, rows)
        stores.append(
            pltpu.make_async_copy(
                out_ref.at[pl.ds(0, planes), span, :], planes_hbm.at[:, span, :], sems.at[k, 0]
            )
        )
        stores.append(pltpu.make_async_copy(out_ref.at[planes, span, :], last_hbm.at[span, :], sems.at[k, 1]))
        stores[-2].start()
        stores[-1].start()
        if k + 1 < len(RESTORE_BLOCKS):
            fill(k + 1)
    for store in stores:
        store.wait()


def restore(perm, data):
    total, width = data.shape
    planes = width // 128 - 1
    out = [
        jax.ShapeDtypeStruct((planes, total, 128), BF16),
        jax.ShapeDtypeStruct((total, 128), BF16),
    ]
    near, far = pl.BlockSpec(memory_space=pltpu.VMEM), pl.BlockSpec(memory_space=pl.ANY)
    scratch = [
        pltpu.VMEM((2, max(RESTORE_BLOCKS), total), BF16),
        pltpu.VMEM((planes + 1, total, 128), BF16),
        pltpu.SemaphoreType.DMA((len(RESTORE_BLOCKS), 2)),
    ]
    flops = 2 * total * total * width
    return call(restore_kernel, out, flops, 40, scratch, [near] * 2, [far] * 2)(perm, data)


ADJOINT_ROWS = 512
SCATTER_ROWS = 1024


def two_hot(index_ref, share_ref, start, rows):
    count = index_ref.shape[1]
    block = 256
    first, second, share = index_ref[0:1, :], index_ref[1:2, :], share_ref[...]
    high = jnp.where(first == second, 1.0, share).astype(BF16)
    low = (1.0 - share).astype(BF16)
    targets = lax.broadcasted_iota(jnp.int32, (block, count), 0).astype(F32).astype(BF16)
    spread = lambda row: jnp.broadcast_to(row, (block, count))
    pieces = []
    for at in range(0, rows, block):
        one = spread((first - (start + at)).astype(F32).astype(BF16)) == targets
        two = spread((second - (start + at)).astype(F32).astype(BF16)) == targets
        pieces.append(jnp.where(one, spread(high), jnp.where(two, spread(low), jnp.zeros((), BF16))))
    return pieces[0] if len(pieces) == 1 else jnp.concatenate(pieces, axis=0)


def radiation_kernel(
    data_ref,
    bidx_ref,
    bw_ref,
    cidx_ref,
    cw_ref,
    scale_ref,
    ta_hbm,
    tb_hbm,
    out_ref,
    table_ref,
    sems,
    back_ref,
    coarse_ref,
    tt_ref,
    rows_ref,
    adj_ref,
    mid_ref,
    heat_ref,
):
    bands, width, _ = table_ref.shape
    cols, rows = coarse_ref.shape
    half = bands // 2
    loads = [
        pltpu.make_async_copy(ta_hbm, table_ref.at[pl.ds(0, half)], sems.at[0]),
        pltpu.make_async_copy(tb_hbm, table_ref.at[pl.ds(half, half)], sems.at[1]),
    ]
    for load in loads:
        load.start()

    def adjoint(i, carry):
        start = pl.multiple_of(i * ADJOINT_ROWS, ADJOINT_ROWS)
        matrix = two_hot(bidx_ref, bw_ref, start, ADJOINT_ROWS)
        back_ref[pl.ds(start, ADJOINT_ROWS), :] = matrix
        adj_ref[:, pl.ds(start, ADJOINT_ROWS)] = jnp.dot(
            matrix, data_ref[:, width:], preferred_element_type=F32
        ).T
        return carry

    lax.fori_loop(0, rows // ADJOINT_ROWS, adjoint, 0)
    for load in loads:
        load.wait()

    lifted = jnp.concatenate(
        [(adj_ref[...] * scale_ref[b : b + 1, :]).astype(BF16) for b in range(bands)], axis=0
    )
    tables = jnp.concatenate([table_ref[b] for b in range(bands)], axis=1)
    rows_ref[...] = jnp.dot(tables, lifted, preferred_element_type=F32).astype(BF16)

    def scatter(i, carry):
        start = pl.multiple_of(i * SCATTER_ROWS, SCATTER_ROWS)
        matrix = two_hot(cidx_ref, cw_ref, start, SCATTER_ROWS)
        coarse_ref[pl.ds(start, SCATTER_ROWS), :] = matrix
        got = lax.dot_general(
            rows_ref[...], matrix, (((1,), (1,)), ((), ())), preferred_element_type=F32
        )
        out_ref[pl.ds(start, SCATTER_ROWS), :width] = got.T.astype(BF16)
        per = bands * SCATTER_ROWS // cols
        for k in range(per):
            b = i * per + k
            tt_ref[:, pl.ds(pl.multiple_of(b * width, 128), width)] = table_ref[b].T
        return carry

    lax.fori_loop(0, cols // SCATTER_ROWS, scatter, 0)

    mid_ref[...] = lax.dot_general(
        data_ref[:, :width], coarse_ref[...], (((0,), (0,)), ((), ())), preferred_element_type=F32
    ).astype(BF16)
    lifted = jnp.concatenate(
        [
            mid_ref[...] * jnp.broadcast_to(scale_ref[b : b + 1, :].astype(BF16), mid_ref.shape)
            for b in range(bands)
        ],
        axis=0,
    )
    heat_ref[...] = jnp.dot(tt_ref[...], lifted, preferred_element_type=F32).astype(BF16)
    tendency = jnp.dot(heat_ref[...], back_ref[...], preferred_element_type=F32)
    out_ref[:, width:] = tendency.T.astype(BF16)


def radiation(data, bidx, bw, cidx, cw, scale, ta, tb):
    cols, rows = bw.shape[1], cw.shape[1]
    bands, width, levels = ta.shape
    out = jax.ShapeDtypeStruct((cols, width + levels), BF16)
    flops = 8 * bands * rows * levels * width
    scratch = [
        pltpu.VMEM((2 * bands, width, levels), BF16),
        pltpu.SemaphoreType.DMA((2,)),
        pltpu.VMEM((rows, cols), BF16),
        pltpu.VMEM((cols, rows), BF16),
        pltpu.VMEM((levels, 2 * bands * width), BF16),
        pltpu.VMEM((width, rows), BF16),
        pltpu.VMEM((levels, rows), F32),
        pltpu.VMEM((width, rows), BF16),
        pltpu.VMEM((levels, rows), BF16),
    ]
    near, far = pl.BlockSpec(memory_space=pltpu.VMEM), pl.BlockSpec(memory_space=pl.ANY)
    specs = [near] * 6 + [far] * 2
    kernel = call(radiation_kernel, out, flops, 34, scratch, specs)
    return kernel(data, bidx, bw, cidx, cw, scale, ta, tb)


def gather_four(block, stride):
    lon = lax.axis_size("lon")
    place = lax.rem(lax.axis_index("lon") // stride, 4)
    size = block.shape[0]
    out = jnp.zeros((4 * size,) + block.shape[1:], block.dtype)
    got = {0: block}
    for shift in (2, 1, 3):
        pairs = []
        for a in range(lon):
            at = a // stride % 4
            pairs.append((a, a + ((at + shift) % 4 - at) * stride))
        got[shift] = lax.ppermute(block, "lon", pairs)
    for shift in (0, 2, 1, 3):
        out = lax.dynamic_update_slice_in_dim(
            out, got[shift], lax.rem(place + 4 - shift, 4) * size, axis=0
        )
    return out


def exchange(values, axes):
    return lax.all_to_all(values, axes, split_axis=0, concat_axis=0, tiled=True)


def local(
    increments,
    cotangent,
    owner_perm,
    coarse_index,
    coarse_weight,
    back_index,
    back_weight,
    lw_scale,
    sw_scale,
    sunlit,
    lw_table,
    sw_table,
):
    lat = lax.axis_size("lat")
    core = lax.rem(lax.axis_index("lat"), 2)
    table = jnp.concatenate([lw_table, sw_table], axis=0)
    bands, _, _, levels = table.shape
    half = bands // 2
    mine = lax.dynamic_slice_in_dim(table, core * half, half, axis=0)
    column = gather_four(mine[None], 1)
    whole = gather_four(column, 4)
    partner = [(a, a + 1 - 2 * (a % 2)) for a in range(lat)]
    other = lax.ppermute(whole, "lat", partner)
    mine, other = (
        t.transpose(1, 2, 0, 3, 4).reshape(half, -1, levels) for t in (whole, other)
    )
    scale = jnp.concatenate([lw_scale, sw_scale * sunlit.astype(F32)[None, :]], axis=0)
    scale = jnp.where(core == 0, scale, jnp.roll(scale, half, axis=0))
    scale = jnp.pad(scale, ((0, 2), (0, 0)))

    cw = coarse_weight[None]
    bw = back_weight[None]
    planes = increments.transpose(1, 0, 2)
    data = pick(owner_perm, planes, cotangent)
    data = exchange(data, ALL)
    back = radiation(data, back_index, bw, coarse_index, cw, scale, mine, other)
    back = exchange(back, ALL)
    gradient, tendency = restore(owner_perm, back)
    return (tendency, gradient.transpose(1, 0, 2))


def solution(mesh):
    in_specs = (
        P(ALL, None, None),
        P(ALL, None),
        P(ALL, None),
        P(None, ALL),
        P(ALL),
        P(None, ALL),
        P(ALL),
        P(None, ALL),
        P(None, ALL),
        P(ALL),
        P(None, None, "lon", None),
        P(None, None, "lon", None),
    )
    out_specs = (P(ALL, None), P(ALL, None, None))
    return jax.shard_map(local, mesh=mesh, in_specs=in_specs, out_specs=out_specs, check_vma=False)
```

profile of v0, /device:TPU:1, one launch (start us, length us, event | category | flops | bytes accessed | tf_op | source)
XLA Modules:
  0.0 126.3 jit_solution(7112476495674999801)
XLA Ops:
  0.6 0.1 broadcast_in_dim.19
  0.7 1.0 constant_dynamic-update-slice_fusion.7
  1.7 3.6 %collective-permute-start = (bf16[1,15,3,8,128]{4,3,0,2,1:T(8,128)(2,1)S(1)}, bf16[1,15,3,8,128]{4,3,0,2,1:T(8,128)(2,1)S(1)}, u32[]{:S(2)}, u32[]{:S(2)}) collective-permute-start(bf16[1,15,3,8,128]{4,3,0,2,1:T(8,128)(2,1)S(1)} %get-tuple-element.7), channel_id=1, source_target_pairs={{0,2},{1,3},{2,0},{3,1},{4,6},{5,7},{6,4},{7,5},{8,10},{9,11},{10,... | collective-permute-start | bytes 276488 | tf_op jit(solution)/shard_map/ppermute | solution.py:275
  5.3 0.3 collective-permute-start.1
  5.6 2.4 %collective-permute-start.2 = (bf16[1,15,3,8,128]{4,3,0,2,1:T(8,128)(2,1)S(1)}, bf16[1,15,3,8,128]{4,3,0,2,1:T(8,128)(2,1)S(1)}, u32[]{:S(2)}, u32[]{:S(2)}) collective-permute-start(bf16[1,15,3,8,128]{4,3,0,2,1:T(8,128)(2,1)S(1)} %get-tuple-element.7), channel_id=1, source_target_pairs={{0,3},{1,0},{2,1},{3,2},{4,7},{5,4},{6,5},{7,6},{8,11},{9,8},{10,9... | collective-permute-start | bytes 276488 | tf_op jit(solution)/shard_map/ppermute | solution.py:275
  8.0 0.0 collective-permute-done
  8.0 1.9 %collective-permute-done.1 = bf16[1,15,3,8,128]{4,3,0,2,1:T(8,128)(2,1)S(1)} collective-permute-done((bf16[1,15,3,8,128]{4,3,0,2,1:T(8,128)(2,1)S(1)}, bf16[1,15,3,8,128]{4,3,0,2,1:T(8,128)(2,1)S(1)}, u32[]{:S(2)}, u32[]{:S(2)}) %collective-permute-start.1) | collective-permute-done | bytes 92192 | tf_op jit(solution)/shard_map/ppermute | solution.py:275
  10.0 0.0 collective-permute-done.2
  10.0 3.0 %collective-permute-start.3 = (bf16[4,15,3,8,128]{4,3,0,2,1:T(8,128)(2,1)S(1)}, bf16[4,15,3,8,128]{4,3,0,2,1:T(8,128)(2,1)}, u32[]{:S(2)}, u32[]{:S(2)}) collective-permute-start(bf16[4,15,3,8,128]{4,3,0,2,1:T(8,128)(2,1)S(1)} %constant_dynamic-update-slice_fusion.4), channel_id=1, source_target_pairs={{0,8},{1,9},{2,10},{3,11},{4,12},{5,13},{6,14},{7,15},{8,0},{9,1},... | collective-permute-start | bytes 1105928 | tf_op jit(solution)/shard_map/ppermute | solution.py:275
  13.0 0.4 collective-permute-start.4
  13.4 6.8 %shard_map.131 = bf16[2048,512]{1,0:T(8,128)(2,1)} custom-call(s32[1,2048]{1,0:T(1,128)} %perm_ref.1, bf16[3,2048,128]{2,1,0:T(8,128)(2,1)} %bitcast.23, bf16[2048,128]{1,0:T(8,128)(2,1)} %last_hbm.1), custom_call_target="tpu_custom_call" | custom-call | flops 4294967296 | bytes 4194304 | tf_op jit(solution)/shard_map/pallas_call | solution.py:88
  20.2 12.2 %all-to-all-start = ((bf16[128,16,512]{2,1,0:T(8,128)(2,1)}), bf16[128,16,512]{2,1,0:T(8,128)(2,1)S(1)}, u32[]{:S(2)}, u32[]{:S(2)}) async-start(bf16[128,16,512]{2,1,0:T(8,128)(2,1)} %bitcast.22), calls=%async_computation | async-start | bytes 4194304 | tf_op jit(solution)/shard_map/all_to_all | solution.py:284
  32.4 2.7 %collective-permute-start.5 = (bf16[4,15,3,8,128]{4,3,0,2,1:T(8,128)(2,1)S(1)}, bf16[4,15,3,8,128]{4,3,0,2,1:T(8,128)(2,1)S(1)}, u32[]{:S(2)}, u32[]{:S(2)}) collective-permute-start(bf16[4,15,3,8,128]{4,3,0,2,1:T(8,128)(2,1)S(1)} %constant_dynamic-update-slice_fusion.4), channel_id=1, source_target_pairs={{0,12},{1,13},{2,14},{3,15},{4,0},{5,1},{6,2},{7,3},{8,4},{9,5},{1... | collective-permute-start | bytes 1105928 | tf_op jit(solution)/shard_map/ppermute | solution.py:275
  35.1 1.5 %broadcast_in_dim.18 = bf16[16,15,3,8,128]{4,3,0,2,1:T(8,128)(2,1)} broadcast(bf16[]{:T(256)} %constant.74.clone.1), dimensions={} | broadcast | bytes 1474562 | tf_op jit(solution)/shard_map/broadcast_in_dim | solution.py:268
  36.6 0.0 copy-start.7
  36.6 0.0 copy-start.6
  36.6 0.0 copy-start.5
  36.6 0.8 constant_dynamic-update-slice_fusion.3
  37.4 0.0 collective-permute-done.3
  37.4 1.8 %constant_dynamic-update-slice_fusion.2 = bf16[16,15,3,8,128]{4,3,0,2,1:T(8,128)(2,1)} fusion(bf16[16,15,3,8,128]{4,3,0,2,1:T(8,128)(2,1)} %constant_dynamic-update-slice_fusion.3, bf16[4,15,3,8,128]{4,3,0,2,1:T(8,128)(2,1)} %collective-permute-done.3, s32[]{:T(128)S(6)} %select_n.50), kind=kLoop, calls=%fused_computation.12 | loop fusion | bytes 737284 | tf_op jit(solution)/shard_map/dynamic_update_slice | solution.py:277
  39.2 0.0 copy-start
  39.2 0.0 copy-start.1
  39.2 0.0 copy-start.2
  39.2 0.0 copy-start.4
  39.2 0.0 collective-permute-done.4
  39.2 0.8 constant_dynamic-update-slice_fusion.1
  40.0 24.1 %collective-permute-done.5 = bf16[4,15,3,8,128]{4,3,0,2,1:T(8,128)(2,1)S(1)} collective-permute-done((bf16[4,15,3,8,128]{4,3,0,2,1:T(8,128)(2,1)S(1)}, bf16[4,15,3,8,128]{4,3,0,2,1:T(8,128)(2,1)S(1)}, u32[]{:S(2)}, u32[]{:S(2)}) %collective-permute-start.5) | collective-permute-done | bytes 368672 | tf_op jit(solution)/shard_map/ppermute | solution.py:275
  64.2 0.8 constant_dynamic-update-slice_fusion
  65.0 1.0 collective-permute-start.6
  65.9 0.0 copy-done.7
  65.9 0.0 copy-done.6
  66.0 0.0 copy-done.5
  66.0 3.1 %collective-permute-done.6 = bf16[16,15,3,8,128]{4,3,0,2,1:T(8,128)(2,1)} collective-permute-done((bf16[16,15,3,8,128]{4,3,0,2,1:T(8,128)(2,1)}, bf16[16,15,3,8,128]{4,3,0,2,1:T(8,128)(2,1)}, u32[]{:S(2)}, u32[]{:S(2)}) %collective-permute-start.6) | collective-permute-done | bytes 1474592 | tf_op jit(solution)/shard_map/ppermute | solution.py:310
  69.2 0.0 all-to-all-done
  69.2 0.0 copy-done
  69.2 0.0 copy-done.1
  69.2 0.0 copy-done.2
  69.2 0.0 copy-done.4
  69.2 12.8 %shard_map.132 = bf16[2048,512]{1,0:T(8,128)(2,1)S(1)} custom-call(bf16[2048,512]{1,0:T(8,128)(2,1)S(1)} %bitcast.17, s32[2,2048]{1,0:T(2,128)S(1)} %copy-done, f32[1,2048]{1,0:T(1,128)S(1)} %bitcast.20, s32[2,1024]{1,0:T(2,128)S(1)} %copy-done.2, f32[1,1024]{1,0:T(1,128)S(1)} %bitcast.21, f32[32,1024]{1,0:T(8,128)S(1)} %pad.4.scale_ref, ...), custom_call_target="tpu_custom_call" | custom-call | flops 6039797760 | bytes 4194304 | tf_op jit(solution)/shard_map/pallas_call | solution.py:261
  82.0 0.0 copy-start.3
  82.0 38.8 %all_to_all.22 = bf16[128,16,512]{2,1,0:T(8,128)(2,1)S(1)} all-to-all(bf16[128,16,512]{2,1,0:T(8,128)(2,1)S(1)} %bitcast.18), channel_id=1, replica_groups=mesh['lat'=8,'lon'=16] {'lat','lon'}, dimensions={0} | all-to-all | bytes 4194304 | tf_op jit(solution)/shard_map/all_to_all | solution.py:284
  120.8 0.0 copy-done.3
  120.8 5.3 %shard_map.133 = (bf16[3,2048,128]{2,1,0:T(8,128)(2,1)}, bf16[2048,128]{1,0:T(8,128)(2,1)}) custom-call(s32[1,2048]{1,0:T(1,128)S(1)} %copy-done.3, bf16[2048,512]{1,0:T(8,128)(2,1)S(1)} %bitcast.19), custom_call_target="tpu_custom_call" | custom-call | flops 4294967296 | bytes 4194304 | tf_op jit(solution)/shard_map/pallas_call | solution.py:139
  (8 shorter events, 0.1 us)
Async XLA Ops:
  1.7 6.3 %collective-permute-start = (bf16[1,15,3,8,128]{4,3,0,2,1:T(8,128)(2,1)S(1)}, bf16[1,15,3,8,128]{4,3,0,2,1:T(8,128)(2,1)S(1)}, u32[]{:S(2)}, u32[]{:S(2)}) collective-permute-start(bf16[1,15,3,8,128]{4,3,0,2,1:T(8,128)(2,1)S(1)} %get-tuple-element.7), channel_id=1, source_target_pairs={{0,2},{1,3},{2,0},{3,1},{4,6},{5,7},{6,4},{7,5},{8,10},{9,11},{10,... | collective-permute-start | bytes 276488 | tf_op jit(solution)/shard_map/ppermute | solution.py:275
  5.3 4.6 %collective-permute-start.1 = (bf16[1,15,3,8,128]{4,3,0,2,1:T(8,128)(2,1)S(1)}, bf16[1,15,3,8,128]{4,3,0,2,1:T(8,128)(2,1)S(1)}, u32[]{:S(2)}, u32[]{:S(2)}) collective-permute-start(bf16[1,15,3,8,128]{4,3,0,2,1:T(8,128)(2,1)S(1)} %get-tuple-element.7), channel_id=1, source_target_pairs={{0,1},{1,2},{2,3},{3,0},{4,5},{5,6},{6,7},{7,4},{8,9},{9,10},{10,1... | collective-permute-start | bytes 276488 | tf_op jit(solution)/shard_map/ppermute | solution.py:275
  5.6 4.3 %collective-permute-start.2 = (bf16[1,15,3,8,128]{4,3,0,2,1:T(8,128)(2,1)S(1)}, bf16[1,15,3,8,128]{4,3,0,2,1:T(8,128)(2,1)S(1)}, u32[]{:S(2)}, u32[]{:S(2)}) collective-permute-start(bf16[1,15,3,8,128]{4,3,0,2,1:T(8,128)(2,1)S(1)} %get-tuple-element.7), channel_id=1, source_target_pairs={{0,3},{1,0},{2,1},{3,2},{4,7},{5,4},{6,5},{7,6},{8,11},{9,8},{10,9... | collective-permute-start | bytes 276488 | tf_op jit(solution)/shard_map/ppermute | solution.py:275
  10.0 27.4 %collective-permute-start.3 = (bf16[4,15,3,8,128]{4,3,0,2,1:T(8,128)(2,1)S(1)}, bf16[4,15,3,8,128]{4,3,0,2,1:T(8,128)(2,1)}, u32[]{:S(2)}, u32[]{:S(2)}) collective-permute-start(bf16[4,15,3,8,128]{4,3,0,2,1:T(8,128)(2,1)S(1)} %constant_dynamic-update-slice_fusion.4), channel_id=1, source_target_pairs={{0,8},{1,9},{2,10},{3,11},{4,12},{5,13},{6,14},{7,15},{8,0},{9,1},... | collective-permute-start | bytes 1105928 | tf_op jit(solution)/shard_map/ppermute | solution.py:275
  13.0 26.2 %collective-permute-start.4 = (bf16[4,15,3,8,128]{4,3,0,2,1:T(8,128)(2,1)S(1)}, bf16[4,15,3,8,128]{4,3,0,2,1:T(8,128)(2,1)S(1)}, u32[]{:S(2)}, u32[]{:S(2)}) collective-permute-start(bf16[4,15,3,8,128]{4,3,0,2,1:T(8,128)(2,1)S(1)} %constant_dynamic-update-slice_fusion.4), channel_id=1, source_target_pairs={{0,4},{1,5},{2,6},{3,7},{4,8},{5,9},{6,10},{7,11},{8,12},{9,13},{1... | collective-permute-start | bytes 1105928 | tf_op jit(solution)/shard_map/ppermute | solution.py:275
  20.2 49.0 %all-to-all-start = ((bf16[128,16,512]{2,1,0:T(8,128)(2,1)}), bf16[128,16,512]{2,1,0:T(8,128)(2,1)S(1)}, u32[]{:S(2)}, u32[]{:S(2)}) async-start(bf16[128,16,512]{2,1,0:T(8,128)(2,1)} %bitcast.22), calls=%async_computation | async-start | bytes 4194304 | tf_op jit(solution)/shard_map/all_to_all | solution.py:284
  32.4 31.7 %collective-permute-start.5 = (bf16[4,15,3,8,128]{4,3,0,2,1:T(8,128)(2,1)S(1)}, bf16[4,15,3,8,128]{4,3,0,2,1:T(8,128)(2,1)S(1)}, u32[]{:S(2)}, u32[]{:S(2)}) collective-permute-start(bf16[4,15,3,8,128]{4,3,0,2,1:T(8,128)(2,1)S(1)} %constant_dynamic-update-slice_fusion.4), channel_id=1, source_target_pairs={{0,12},{1,13},{2,14},{3,15},{4,0},{5,1},{6,2},{7,3},{8,4},{9,5},{1... | collective-permute-start | bytes 1105928 | tf_op jit(solution)/shard_map/ppermute | solution.py:275
  36.6 29.4 %copy-start.7 = (s32[1024]{0:T(1024)S(1)}, s32[1024]{0:T(1024)}, u32[]{:S(2)}) copy-start(s32[1024]{0:T(1024)} %param.21) | copy-start | bytes 12292
  36.6 29.4 %copy-start.6 = (f32[14,1024]{1,0:T(8,128)S(1)}, f32[14,1024]{1,0:T(8,128)}, u32[]{:S(2)}) copy-start(f32[14,1024]{1,0:T(8,128)} %param.20) | copy-start | bytes 172036
  36.6 29.4 %copy-start.5 = (f32[16,1024]{1,0:T(8,128)S(1)}, f32[16,1024]{1,0:T(8,128)}, u32[]{:S(2)}) copy-start(f32[16,1024]{1,0:T(8,128)} %param.19) | copy-start | bytes 196612
  39.2 30.0 %copy-start = (s32[2,2048]{1,0:T(2,128)S(1)}, s32[2,2048]{1,0:T(2,128)}, u32[]{:S(2)}) copy-start(s32[2,2048]{1,0:T(2,128)} %bidx_ref.1) | copy-start | bytes 49156
  39.2 30.0 %copy-start.1 = (f32[2048]{0:T(1024)S(1)}, f32[2048]{0:T(1024)}, u32[]{:S(2)}) copy-start(f32[2048]{0:T(1024)} %param.18) | copy-start | bytes 24580
  39.2 30.0 %copy-start.2 = (s32[2,1024]{1,0:T(2,128)S(1)}, s32[2,1024]{1,0:T(2,128)}, u32[]{:S(2)}) copy-start(s32[2,1024]{1,0:T(2,128)} %cidx_ref.1) | copy-start | bytes 24580
  39.2 30.0 %copy-start.4 = (f32[1024]{0:T(1024)S(1)}, f32[1024]{0:T(1024)}, u32[]{:S(2)}) copy-start(f32[1024]{0:T(1024)} %param.16) | copy-start | bytes 12292
  65.0 4.2 %collective-permute-start.6 = (bf16[16,15,3,8,128]{4,3,0,2,1:T(8,128)(2,1)}, bf16[16,15,3,8,128]{4,3,0,2,1:T(8,128)(2,1)}, u32[]{:S(2)}, u32[]{:S(2)}) collective-permute-start(bf16[16,15,3,8,128]{4,3,0,2,1:T(8,128)(2,1)} %constant_dynamic-update-slice_fusion), channel_id=1, source_target_pairs={{0,16},{16,0},{32,48},{48,32},{64,80},{80,64},{96,112},{112,96},{1... | collective-permute-start | bytes 4423688 | tf_op jit(solution)/shard_map/ppermute | solution.py:310
  82.0 38.8 %copy-start.3 = (s32[1,2048]{1,0:T(1,128)S(1)}, s32[1,2048]{1,0:T(1,128)}, u32[]{:S(2)}) copy-start(s32[1,2048]{1,0:T(1,128)} %perm_ref.1) | copy-start | bytes 24580
where the time goes:
time: 127 us; the launch traced here: 126 us
  blocking collectives  38.8 us (31%)
  waiting for transfers between devices  29.2 us (23%)
  starting transfers between devices  25.6 us (20%)
  Pallas kernels  24.9 us (20%)
  local copies, waits for them, and re-layouts  5.84 us (5%)
    all_to_all x1, blocking collectives, exchange(): return lax.all_to_all(values, axes, split_axis=0, concat_axis=0, tiled=True)  38.8 us
    ppermute x6, waiting for transfers between devices, gather_four(): got[shift] = lax.ppermute(block, 'lon', pairs)  26.1 us
    pallas_call x1, Pallas kernels, radiation(): return kernel(data, bidx, bw, cidx, cw, scale, ta, tb)  12.8 us
    ppermute x6, starting transfers between devices, gather_four(): got[shift] = lax.ppermute(block, 'lon', pairs)  12.4 us
    all_to_all x1, starting transfers between devices, exchange(): return lax.all_to_all(values, axes, split_axis=0, concat_axis=0, tiled=True)  12.2 us
    pallas_call x1, Pallas kernels, pick(): call(pick_kernel, out, flops, 60, scratch, [far] * 3, far)  6.82 us
    pallas_call x1, Pallas kernels, restore(): call(restore_kernel, out, flops, 40, scratch, [near] * 2, [far] * 2)  5.25 us
    dynamic_update_slice x7, local copies, waits for them, and re-layouts, gather_four(): lax.dynamic_update_slice_in_dim(out, got[shift], lax.rem(place + 4 - shif...  4.29 us
  transfers between devices with their start and end apart: 8, of which 3 were waited for; matrix products, arithmetic and copies ran while one was open for 5% of the time, Pallas kernels for 5%

commit v1 on v0

--- a/solution.py
+++ b/solution.py
@@ -266,16 +266,16 @@
     place = lax.rem(lax.axis_index("lon") // stride, 4)
     size = block.shape[0]
     out = jnp.zeros((4 * size,) + block.shape[1:], block.dtype)
-    got = {0: block}
-    for shift in (2, 1, 3):
+    got = [block]
+    for shift in (1, 3, 2):
         pairs = []
         for a in range(lon):
             at = a // stride % 4
             pairs.append((a, a + ((at + shift) % 4 - at) * stride))
-        got[shift] = lax.ppermute(block, "lon", pairs)
-    for shift in (0, 2, 1, 3):
+        got.append(lax.ppermute(block, "lon", pairs))
+    for shift, piece in zip((0, 1, 3, 2), got):
         out = lax.dynamic_update_slice_in_dim(
-            out, got[shift], lax.rem(place + 4 - shift, 4) * size, axis=0
+            out, piece, lax.rem(place + 4 - shift, 4) * size, axis=0
         )
     return out
 

time: 127 us -> 124 us (0.976)
  starting transfers between devices: 25.6 us -> 22.1 us
  waiting for transfers between devices: 29.2 us -> 32 us
  blocking collectives: 38.8 us -> 37.2 us
    ppermute x6, waiting for transfers between devices: 26.1 us -> 28.9 us  [gather_four(): got.append(lax.ppermute(block, 'lon', pairs))]
    all_to_all x1, starting transfers between devices: 12.2 us -> 10.2 us  [exchange(): return lax.all_to_all(values, axes, split_axis=0, concat_axis=0, tiled=True)]
    all_to_all x1, blocking collectives: 38.8 us -> 37.2 us  [exchange(): return lax.all_to_all(values, axes, split_axis=0, concat_axis=0, tiled=True)]
    ppermute x6, starting transfers between devices: 12.4 us -> 10.9 us  [gather_four(): got.append(lax.ppermute(block, 'lon', pairs))]
  transfers between devices with their start and end apart: 8 -> 8, of which waited for: 3 -> 5; matrix products, arithmetic and copies ran while one was open for 5% -> 5% of each run, Pallas kernels for 5% -> 5%
where the time goes in v1:
time: 124 us
  blocking collectives  37.2 us (30%)
  waiting for transfers between devices  32 us (26%)
  Pallas kernels  24.9 us (20%)
  starting transfers between devices  22.1 us (18%)
  local copies, waits for them, and re-layouts  5.83 us (5%)
    all_to_all x1, blocking collectives, exchange(): return lax.all_to_all(values, axes, split_axis=0, concat_axis=0, tiled=True)  37.2 us
    ppermute x6, waiting for transfers between devices, gather_four(): got.append(lax.ppermute(block, 'lon', pairs))  28.9 us
    pallas_call x1, Pallas kernels, radiation(): return kernel(data, bidx, bw, cidx, cw, scale, ta, tb)  12.8 us
    ppermute x6, starting transfers between devices, gather_four(): got.append(lax.ppermute(block, 'lon', pairs))  10.9 us
    all_to_all x1, starting transfers between devices, exchange(): return lax.all_to_all(values, axes, split_axis=0, concat_axis=0, tiled=True)  10.2 us
    pallas_call x1, Pallas kernels, pick(): call(pick_kernel, out, flops, 60, scratch, [far] * 3, far)  6.82 us
    pallas_call x1, Pallas kernels, restore(): call(restore_kernel, out, flops, 40, scratch, [near] * 2, [far] * 2)  5.25 us
    dynamic_update_slice x7, local copies, waits for them, and re-layouts, gather_four(): lax.dynamic_update_slice_in_dim(out, piece, lax.rem(place + 4 - shift, 4)...  4.28 us
  transfers between devices with their start and end apart: 8, of which 5 were waited for; matrix products, arithmetic and copies ran while one was open for 5% of the time, Pallas kernels for 5%

profile of v1, /device:TPU:1, one launch (start us, length us, event | category | flops | bytes accessed | tf_op | source)
XLA Modules:
  0.0 124.0 jit_solution(17325233440167735527)
XLA Ops:
  0.6 0.1 broadcast_in_dim.19
  0.7 1.0 constant_dynamic-update-slice_fusion.7
  1.7 2.1 %collective-permute-start = (bf16[1,15,3,8,128]{4,3,0,2,1:T(8,128)(2,1)S(1)}, bf16[1,15,3,8,128]{4,3,0,2,1:T(8,128)(2,1)S(1)}, u32[]{:S(2)}, u32[]{:S(2)}) collective-permute-start(bf16[1,15,3,8,128]{4,3,0,2,1:T(8,128)(2,1)S(1)} %get-tuple-element.7), channel_id=1, source_target_pairs={{0,1},{1,2},{2,3},{3,0},{4,5},{5,6},{6,7},{7,4},{8,9},{9,10},{10,1... | collective-permute-start | bytes 276488 | tf_op jit(solution)/shard_map/ppermute | solution.py:275
  3.8 1.3 %collective-permute-start.1 = (bf16[1,15,3,8,128]{4,3,0,2,1:T(8,128)(2,1)S(1)}, bf16[1,15,3,8,128]{4,3,0,2,1:T(8,128)(2,1)S(1)}, u32[]{:S(2)}, u32[]{:S(2)}) collective-permute-start(bf16[1,15,3,8,128]{4,3,0,2,1:T(8,128)(2,1)S(1)} %get-tuple-element.7), channel_id=1, source_target_pairs={{0,3},{1,0},{2,1},{3,2},{4,7},{5,4},{6,5},{7,6},{8,11},{9,8},{10,9... | collective-permute-start | bytes 276488 | tf_op jit(solution)/shard_map/ppermute | solution.py:275
  5.1 1.6 %collective-permute-start.2 = (bf16[1,15,3,8,128]{4,3,0,2,1:T(8,128)(2,1)S(1)}, bf16[1,15,3,8,128]{4,3,0,2,1:T(8,128)(2,1)S(1)}, u32[]{:S(2)}, u32[]{:S(2)}) collective-permute-start(bf16[1,15,3,8,128]{4,3,0,2,1:T(8,128)(2,1)S(1)} %get-tuple-element.7), channel_id=1, source_target_pairs={{0,2},{1,3},{2,0},{3,1},{4,6},{5,7},{6,4},{7,5},{8,10},{9,11},{10,... | collective-permute-start | bytes 276488 | tf_op jit(solution)/shard_map/ppermute | solution.py:275
  6.8 0.2 collective-permute-done
  7.0 0.2 collective-permute-done.1
  7.2 3.1 %collective-permute-done.2 = bf16[1,15,3,8,128]{4,3,0,2,1:T(8,128)(2,1)S(1)} collective-permute-done((bf16[1,15,3,8,128]{4,3,0,2,1:T(8,128)(2,1)S(1)}, bf16[1,15,3,8,128]{4,3,0,2,1:T(8,128)(2,1)S(1)}, u32[]{:S(2)}, u32[]{:S(2)}) %collective-permute-start.2) | collective-permute-done | bytes 92192 | tf_op jit(solution)/shard_map/ppermute | solution.py:275
  10.3 1.4 %collective-permute-start.3 = (bf16[4,15,3,8,128]{4,3,0,2,1:T(8,128)(2,1)S(1)}, bf16[4,15,3,8,128]{4,3,0,2,1:T(8,128)(2,1)}, u32[]{:S(2)}, u32[]{:S(2)}) collective-permute-start(bf16[4,15,3,8,128]{4,3,0,2,1:T(8,128)(2,1)S(1)} %constant_dynamic-update-slice_fusion.4), channel_id=1, source_target_pairs={{0,4},{1,5},{2,6},{3,7},{4,8},{5,9},{6,10},{7,11},{8,12},{9,13},{1... | collective-permute-start | bytes 1105928 | tf_op jit(solution)/shard_map/ppermute | solution.py:275
  11.7 1.5 %collective-permute-start.4 = (bf16[4,15,3,8,128]{4,3,0,2,1:T(8,128)(2,1)S(1)}, bf16[4,15,3,8,128]{4,3,0,2,1:T(8,128)(2,1)S(1)}, u32[]{:S(2)}, u32[]{:S(2)}) collective-permute-start(bf16[4,15,3,8,128]{4,3,0,2,1:T(8,128)(2,1)S(1)} %constant_dynamic-update-slice_fusion.4), channel_id=1, source_target_pairs={{0,12},{1,13},{2,14},{3,15},{4,0},{5,1},{6,2},{7,3},{8,4},{9,5},{1... | collective-permute-start | bytes 1105928 | tf_op jit(solution)/shard_map/ppermute | solution.py:275
  13.2 6.8 %shard_map.131 = bf16[2048,512]{1,0:T(8,128)(2,1)} custom-call(s32[1,2048]{1,0:T(1,128)} %perm_ref.1, bf16[3,2048,128]{2,1,0:T(8,128)(2,1)} %bitcast.23, bf16[2048,128]{1,0:T(8,128)(2,1)} %last_hbm.1), custom_call_target="tpu_custom_call" | custom-call | flops 4294967296 | bytes 4194304 | tf_op jit(solution)/shard_map/pallas_call | solution.py:88
  20.0 10.2 %all-to-all-start = ((bf16[128,16,512]{2,1,0:T(8,128)(2,1)}), bf16[128,16,512]{2,1,0:T(8,128)(2,1)S(1)}, u32[]{:S(2)}, u32[]{:S(2)}) async-start(bf16[128,16,512]{2,1,0:T(8,128)(2,1)} %bitcast.22), calls=%async_computation | async-start | bytes 4194304 | tf_op jit(solution)/shard_map/all_to_all | solution.py:284
  30.3 2.9 %collective-permute-start.5 = (bf16[4,15,3,8,128]{4,3,0,2,1:T(8,128)(2,1)S(1)}, bf16[4,15,3,8,128]{4,3,0,2,1:T(8,128)(2,1)S(1)}, u32[]{:S(2)}, u32[]{:S(2)}) collective-permute-start(bf16[4,15,3,8,128]{4,3,0,2,1:T(8,128)(2,1)S(1)} %constant_dynamic-update-slice_fusion.4), channel_id=1, source_target_pairs={{0,8},{1,9},{2,10},{3,11},{4,12},{5,13},{6,14},{7,15},{8,0},{9,1},... | collective-permute-start | bytes 1105928 | tf_op jit(solution)/shard_map/ppermute | solution.py:275
  33.2 1.5 %broadcast_in_dim.18 = bf16[16,15,3,8,128]{4,3,0,2,1:T(8,128)(2,1)} broadcast(bf16[]{:T(256)} %constant.74.clone.1), dimensions={} | broadcast | bytes 1474562 | tf_op jit(solution)/shard_map/broadcast_in_dim | solution.py:268
  34.7 0.0 copy-start.7
  34.7 0.0 copy-start.6
  34.7 0.0 copy-start.5
  34.7 0.8 constant_dynamic-update-slice_fusion.3
  35.5 0.0 collective-permute-done.3
  35.5 1.8 %constant_dynamic-update-slice_fusion.2 = bf16[16,15,3,8,128]{4,3,0,2,1:T(8,128)(2,1)} fusion(bf16[16,15,3,8,128]{4,3,0,2,1:T(8,128)(2,1)} %constant_dynamic-update-slice_fusion.3, bf16[4,15,3,8,128]{4,3,0,2,1:T(8,128)(2,1)} %collective-permute-done.3, s32[]{:T(128)S(6)} %select_n.50), kind=kLoop, calls=%fused_computation.12 | loop fusion | bytes 737284 | tf_op jit(solution)/shard_map/dynamic_update_slice | solution.py:277
  37.3 0.0 copy-start
  37.3 0.0 copy-start.1
  37.3 0.0 copy-start.2
  37.3 0.0 copy-start.4
  37.3 0.0 collective-permute-done.4
  37.3 0.8 constant_dynamic-update-slice_fusion.1
  38.1 25.4 %collective-permute-done.5 = bf16[4,15,3,8,128]{4,3,0,2,1:T(8,128)(2,1)S(1)} collective-permute-done((bf16[4,15,3,8,128]{4,3,0,2,1:T(8,128)(2,1)S(1)}, bf16[4,15,3,8,128]{4,3,0,2,1:T(8,128)(2,1)S(1)}, u32[]{:S(2)}, u32[]{:S(2)}) %collective-permute-start.5) | collective-permute-done | bytes 368672 | tf_op jit(solution)/shard_map/ppermute | solution.py:275
  63.5 0.8 constant_dynamic-update-slice_fusion
  64.3 1.0 collective-permute-start.6
  65.3 0.0 copy-done.7
  65.3 0.0 copy-done.6
  65.3 0.0 copy-done.5
  65.4 3.1 %collective-permute-done.6 = bf16[16,15,3,8,128]{4,3,0,2,1:T(8,128)(2,1)} collective-permute-done((bf16[16,15,3,8,128]{4,3,0,2,1:T(8,128)(2,1)}, bf16[16,15,3,8,128]{4,3,0,2,1:T(8,128)(2,1)}, u32[]{:S(2)}, u32[]{:S(2)}) %collective-permute-start.6) | collective-permute-done | bytes 1474592 | tf_op jit(solution)/shard_map/ppermute | solution.py:310
  68.5 0.0 all-to-all-done
  68.5 0.0 copy-done
  68.5 0.0 copy-done.1
  68.5 0.0 copy-done.2
  68.5 0.0 copy-done.4
  68.6 12.8 %shard_map.132 = bf16[2048,512]{1,0:T(8,128)(2,1)S(1)} custom-call(bf16[2048,512]{1,0:T(8,128)(2,1)S(1)} %bitcast.17, s32[2,2048]{1,0:T(2,128)S(1)} %copy-done, f32[1,2048]{1,0:T(1,128)S(1)} %bitcast.20, s32[2,1024]{1,0:T(2,128)S(1)} %copy-done.2, f32[1,1024]{1,0:T(1,128)S(1)} %bitcast.21, f32[32,1024]{1,0:T(8,128)S(1)} %pad.4.scale_ref, ...), custom_call_target="tpu_custom_call" | custom-call | flops 6039797760 | bytes 4194304 | tf_op jit(solution)/shard_map/pallas_call | solution.py:261
  81.4 0.0 copy-start.3
  81.4 37.2 %all_to_all.22 = bf16[128,16,512]{2,1,0:T(8,128)(2,1)S(1)} all-to-all(bf16[128,16,512]{2,1,0:T(8,128)(2,1)S(1)} %bitcast.18), channel_id=1, replica_groups=mesh['lat'=8,'lon'=16] {'lat','lon'}, dimensions={0} | all-to-all | bytes 4194304 | tf_op jit(solution)/shard_map/all_to_all | solution.py:284
  118.6 0.0 copy-done.3
  118.6 5.3 %shard_map.133 = (bf16[3,2048,128]{2,1,0:T(8,128)(2,1)}, bf16[2048,128]{1,0:T(8,128)(2,1)}) custom-call(s32[1,2048]{1,0:T(1,128)S(1)} %copy-done.3, bf16[2048,512]{1,0:T(8,128)(2,1)S(1)} %bitcast.19), custom_call_target="tpu_custom_call" | custom-call | flops 4294967296 | bytes 4194304 | tf_op jit(solution)/shard_map/pallas_call | solution.py:139
  (8 shorter events, 0.1 us)
Async XLA Ops:
  1.7 5.3 %collective-permute-start = (bf16[1,15,3,8,128]{4,3,0,2,1:T(8,128)(2,1)S(1)}, bf16[1,15,3,8,128]{4,3,0,2,1:T(8,128)(2,1)S(1)}, u32[]{:S(2)}, u32[]{:S(2)}) collective-permute-start(bf16[1,15,3,8,128]{4,3,0,2,1:T(8,128)(2,1)S(1)} %get-tuple-element.7), channel_id=1, source_target_pairs={{0,1},{1,2},{2,3},{3,0},{4,5},{5,6},{6,7},{7,4},{8,9},{9,10},{10,1... | collective-permute-start | bytes 276488 | tf_op jit(solution)/shard_map/ppermute | solution.py:275
  3.8 3.4 %collective-permute-start.1 = (bf16[1,15,3,8,128]{4,3,0,2,1:T(8,128)(2,1)S(1)}, bf16[1,15,3,8,128]{4,3,0,2,1:T(8,128)(2,1)S(1)}, u32[]{:S(2)}, u32[]{:S(2)}) collective-permute-start(bf16[1,15,3,8,128]{4,3,0,2,1:T(8,128)(2,1)S(1)} %get-tuple-element.7), channel_id=1, source_target_pairs={{0,3},{1,0},{2,1},{3,2},{4,7},{5,4},{6,5},{7,6},{8,11},{9,8},{10,9... | collective-permute-start | bytes 276488 | tf_op jit(solution)/shard_map/ppermute | solution.py:275
  5.1 5.2 %collective-permute-start.2 = (bf16[1,15,3,8,128]{4,3,0,2,1:T(8,128)(2,1)S(1)}, bf16[1,15,3,8,128]{4,3,0,2,1:T(8,128)(2,1)S(1)}, u32[]{:S(2)}, u32[]{:S(2)}) collective-permute-start(bf16[1,15,3,8,128]{4,3,0,2,1:T(8,128)(2,1)S(1)} %get-tuple-element.7), channel_id=1, source_target_pairs={{0,2},{1,3},{2,0},{3,1},{4,6},{5,7},{6,4},{7,5},{8,10},{9,11},{10,... | collective-permute-start | bytes 276488 | tf_op jit(solution)/shard_map/ppermute | solution.py:275
  10.3 25.2 %collective-permute-start.3 = (bf16[4,15,3,8,128]{4,3,0,2,1:T(8,128)(2,1)S(1)}, bf16[4,15,3,8,128]{4,3,0,2,1:T(8,128)(2,1)}, u32[]{:S(2)}, u32[]{:S(2)}) collective-permute-start(bf16[4,15,3,8,128]{4,3,0,2,1:T(8,128)(2,1)S(1)} %constant_dynamic-update-slice_fusion.4), channel_id=1, source_target_pairs={{0,4},{1,5},{2,6},{3,7},{4,8},{5,9},{6,10},{7,11},{8,12},{9,13},{1... | collective-permute-start | bytes 1105928 | tf_op jit(solution)/shard_map/ppermute | solution.py:275
  11.7 25.6 %collective-permute-start.4 = (bf16[4,15,3,8,128]{4,3,0,2,1:T(8,128)(2,1)S(1)}, bf16[4,15,3,8,128]{4,3,0,2,1:T(8,128)(2,1)S(1)}, u32[]{:S(2)}, u32[]{:S(2)}) collective-permute-start(bf16[4,15,3,8,128]{4,3,0,2,1:T(8,128)(2,1)S(1)} %constant_dynamic-update-slice_fusion.4), channel_id=1, source_target_pairs={{0,12},{1,13},{2,14},{3,15},{4,0},{5,1},{6,2},{7,3},{8,4},{9,5},{1... | collective-permute-start | bytes 1105928 | tf_op jit(solution)/shard_map/ppermute | solution.py:275
  20.0 48.5 %all-to-all-start = ((bf16[128,16,512]{2,1,0:T(8,128)(2,1)}), bf16[128,16,512]{2,1,0:T(8,128)(2,1)S(1)}, u32[]{:S(2)}, u32[]{:S(2)}) async-start(bf16[128,16,512]{2,1,0:T(8,128)(2,1)} %bitcast.22), calls=%async_computation | async-start | bytes 4194304 | tf_op jit(solution)/shard_map/all_to_all | solution.py:284
  30.3 33.2 %collective-permute-start.5 = (bf16[4,15,3,8,128]{4,3,0,2,1:T(8,128)(2,1)S(1)}, bf16[4,15,3,8,128]{4,3,0,2,1:T(8,128)(2,1)S(1)}, u32[]{:S(2)}, u32[]{:S(2)}) collective-permute-start(bf16[4,15,3,8,128]{4,3,0,2,1:T(8,128)(2,1)S(1)} %constant_dynamic-update-slice_fusion.4), channel_id=1, source_target_pairs={{0,8},{1,9},{2,10},{3,11},{4,12},{5,13},{6,14},{7,15},{8,0},{9,1},... | collective-permute-start | bytes 1105928 | tf_op jit(solution)/shard_map/ppermute | solution.py:275
  34.7 30.6 %copy-start.7 = (s32[1024]{0:T(1024)S(1)}, s32[1024]{0:T(1024)}, u32[]{:S(2)}) copy-start(s32[1024]{0:T(1024)} %param.21) | copy-start | bytes 12292
  34.7 30.6 %copy-start.6 = (f32[14,1024]{1,0:T(8,128)S(1)}, f32[14,1024]{1,0:T(8,128)}, u32[]{:S(2)}) copy-start(f32[14,1024]{1,0:T(8,128)} %param.20) | copy-start | bytes 172036
  34.7 30.6 %copy-start.5 = (f32[16,1024]{1,0:T(8,128)S(1)}, f32[16,1024]{1,0:T(8,128)}, u32[]{:S(2)}) copy-start(f32[16,1024]{1,0:T(8,128)} %param.19) | copy-start | bytes 196612
  37.3 31.3 %copy-start = (s32[2,2048]{1,0:T(2,128)S(1)}, s32[2,2048]{1,0:T(2,128)}, u32[]{:S(2)}) copy-start(s32[2,2048]{1,0:T(2,128)} %bidx_ref.1) | copy-start | bytes 49156
  37.3 31.3 %copy-start.1 = (f32[2048]{0:T(1024)S(1)}, f32[2048]{0:T(1024)}, u32[]{:S(2)}) copy-start(f32[2048]{0:T(1024)} %param.18) | copy-start | bytes 24580
  37.3 31.3 %copy-start.2 = (s32[2,1024]{1,0:T(2,128)S(1)}, s32[2,1024]{1,0:T(2,128)}, u32[]{:S(2)}) copy-start(s32[2,1024]{1,0:T(2,128)} %cidx_ref.1) | copy-start | bytes 24580
  37.3 31.3 %copy-start.4 = (f32[1024]{0:T(1024)S(1)}, f32[1024]{0:T(1024)}, u32[]{:S(2)}) copy-start(f32[1024]{0:T(1024)} %param.16) | copy-start | bytes 12292
  64.3 4.2 %collective-permute-start.6 = (bf16[16,15,3,8,128]{4,3,0,2,1:T(8,128)(2,1)}, bf16[16,15,3,8,128]{4,3,0,2,1:T(8,128)(2,1)}, u32[]{:S(2)}, u32[]{:S(2)}) collective-permute-start(bf16[16,15,3,8,128]{4,3,0,2,1:T(8,128)(2,1)} %constant_dynamic-update-slice_fusion), channel_id=1, source_target_pairs={{0,16},{16,0},{32,48},{48,32},{64,80},{80,64},{96,112},{112,96},{1... | collective-permute-start | bytes 4423688 | tf_op jit(solution)/shard_map/ppermute | solution.py:310
  81.4 37.2 %copy-start.3 = (s32[1,2048]{1,0:T(1,128)S(1)}, s32[1,2048]{1,0:T(1,128)}, u32[]{:S(2)}) copy-start(s32[1,2048]{1,0:T(1,128)} %perm_ref.1) | copy-start | bytes 24580

commit v2 on v1

--- a/solution.py
+++ b/solution.py
@@ -52,13 +52,16 @@
         hot_ref[k % 2, :rows, :] = hot.astype(F32).astype(BF16)
 
     fill(0)
-    for load in loads:
-        load.wait()
     stores = []
     for k, (start, rows) in enumerate(zip(starts(PICK_BLOCKS), PICK_BLOCKS)):
-        data = jnp.concatenate([data_ref[v] for v in range(planes + 1)], axis=1)
-        got = jnp.dot(hot_ref[k % 2, :rows, :], data, preferred_element_type=F32)
-        out_ref[start : start + rows, :] = got.astype(BF16)
+        step = 2 if k == 0 else planes + 1
+        for v in range(0, planes + 1, step):
+            if k == 0:
+                for load in loads[v : v + step]:
+                    load.wait()
+            data = jnp.concatenate([data_ref[u] for u in range(v, v + step)], axis=1)
+            got = jnp.dot(hot_ref[k % 2, :rows, :], data, preferred_element_type=F32)
+            out_ref[start : start + rows, v * 128 : (v + step) * 128] = got.astype(BF16)
         stores.append(
             pltpu.make_async_copy(
                 out_ref.at[pl.ds(start, rows), :], out_hbm.at[pl.ds(start, rows), :], out_sems.at[k]

time: 124 us -> 125 us (level)
  transfers between devices with their start and end apart: 8 -> 8, of which waited for: 5 -> 5; matrix products, arithmetic and copies ran while one was open for 5% -> 5% of each run, Pallas kernels for 5% -> 6%
where the time goes in v2:
time: 125 us; the launch traced here: 124 us
  blocking collectives  37.2 us (30%)
  waiting for transfers between devices  32 us (26%)
  Pallas kernels  25.3 us (20%)
  starting transfers between devices  22.2 us (18%)
  local copies, waits for them, and re-layouts  5.83 us (5%)
    all_to_all x1, blocking collectives, exchange(): return lax.all_to_all(values, axes, split_axis=0, concat_axis=0, tiled=True)  37.2 us
    ppermute x6, waiting for transfers between devices, gather_four(): got.append(lax.ppermute(block, 'lon', pairs))  28.9 us
    pallas_call x1, Pallas kernels, radiation(): return kernel(data, bidx, bw, cidx, cw, scale, ta, tb)  12.8 us
    ppermute x6, starting transfers between devices, gather_four(): got.append(lax.ppermute(block, 'lon', pairs))  10.9 us
    all_to_all x1, starting transfers between devices, exchange(): return lax.all_to_all(values, axes, split_axis=0, concat_axis=0, tiled=True)  10.3 us
    pallas_call x1, Pallas kernels, pick(): call(pick_kernel, out, flops, 60, scratch, [far] * 3, far)  7.21 us
    pallas_call x1, Pallas kernels, restore(): call(restore_kernel, out, flops, 40, scratch, [near] * 2, [far] * 2)  5.25 us
    dynamic_update_slice x7, local copies, waits for them, and re-layouts, gather_four(): lax.dynamic_update_slice_in_dim(out, piece, lax.rem(place + 4 - shift, 4)...  4.28 us
  transfers between devices with their start and end apart: 8, of which 5 were waited for; matrix products, arithmetic and copies ran while one was open for 5% of the time, Pallas kernels for 6%

profile of v2, /device:TPU:1, one launch (start us, length us, event | category | flops | bytes accessed | tf_op | source)
XLA Modules:
  0.0 124.4 jit_solution(858452518297913474)
XLA Ops:
  0.6 0.1 broadcast_in_dim.19
  0.7 1.0 constant_dynamic-update-slice_fusion.7
  1.7 2.1 %collective-permute-start = (bf16[1,15,3,8,128]{4,3,0,2,1:T(8,128)(2,1)S(1)}, bf16[1,15,3,8,128]{4,3,0,2,1:T(8,128)(2,1)S(1)}, u32[]{:S(2)}, u32[]{:S(2)}) collective-permute-start(bf16[1,15,3,8,128]{4,3,0,2,1:T(8,128)(2,1)S(1)} %get-tuple-element.7), channel_id=1, source_target_pairs={{0,1},{1,2},{2,3},{3,0},{4,5},{5,6},{6,7},{7,4},{8,9},{9,10},{10,1... | collective-permute-start | bytes 276488 | tf_op jit(solution)/shard_map/ppermute | solution.py:278
  3.8 1.3 %collective-permute-start.1 = (bf16[1,15,3,8,128]{4,3,0,2,1:T(8,128)(2,1)S(1)}, bf16[1,15,3,8,128]{4,3,0,2,1:T(8,128)(2,1)S(1)}, u32[]{:S(2)}, u32[]{:S(2)}) collective-permute-start(bf16[1,15,3,8,128]{4,3,0,2,1:T(8,128)(2,1)S(1)} %get-tuple-element.7), channel_id=1, source_target_pairs={{0,3},{1,0},{2,1},{3,2},{4,7},{5,4},{6,5},{7,6},{8,11},{9,8},{10,9... | collective-permute-start | bytes 276488 | tf_op jit(solution)/shard_map/ppermute | solution.py:278
  5.1 1.6 %collective-permute-start.2 = (bf16[1,15,3,8,128]{4,3,0,2,1:T(8,128)(2,1)S(1)}, bf16[1,15,3,8,128]{4,3,0,2,1:T(8,128)(2,1)S(1)}, u32[]{:S(2)}, u32[]{:S(2)}) collective-permute-start(bf16[1,15,3,8,128]{4,3,0,2,1:T(8,128)(2,1)S(1)} %get-tuple-element.7), channel_id=1, source_target_pairs={{0,2},{1,3},{2,0},{3,1},{4,6},{5,7},{6,4},{7,5},{8,10},{9,11},{10,... | collective-permute-start | bytes 276488 | tf_op jit(solution)/shard_map/ppermute | solution.py:278
  6.8 0.2 collective-permute-done
  7.0 0.2 collective-permute-done.1
  7.2 3.1 %collective-permute-done.2 = bf16[1,15,3,8,128]{4,3,0,2,1:T(8,128)(2,1)S(1)} collective-permute-done((bf16[1,15,3,8,128]{4,3,0,2,1:T(8,128)(2,1)S(1)}, bf16[1,15,3,8,128]{4,3,0,2,1:T(8,128)(2,1)S(1)}, u32[]{:S(2)}, u32[]{:S(2)}) %collective-permute-start.2) | collective-permute-done | bytes 92192 | tf_op jit(solution)/shard_map/ppermute | solution.py:278
  10.3 1.4 %collective-permute-start.3 = (bf16[4,15,3,8,128]{4,3,0,2,1:T(8,128)(2,1)S(1)}, bf16[4,15,3,8,128]{4,3,0,2,1:T(8,128)(2,1)}, u32[]{:S(2)}, u32[]{:S(2)}) collective-permute-start(bf16[4,15,3,8,128]{4,3,0,2,1:T(8,128)(2,1)S(1)} %constant_dynamic-update-slice_fusion.4), channel_id=1, source_target_pairs={{0,4},{1,5},{2,6},{3,7},{4,8},{5,9},{6,10},{7,11},{8,12},{9,13},{1... | collective-permute-start | bytes 1105928 | tf_op jit(solution)/shard_map/ppermute | solution.py:278
  11.7 1.5 %collective-permute-start.4 = (bf16[4,15,3,8,128]{4,3,0,2,1:T(8,128)(2,1)S(1)}, bf16[4,15,3,8,128]{4,3,0,2,1:T(8,128)(2,1)S(1)}, u32[]{:S(2)}, u32[]{:S(2)}) collective-permute-start(bf16[4,15,3,8,128]{4,3,0,2,1:T(8,128)(2,1)S(1)} %constant_dynamic-update-slice_fusion.4), channel_id=1, source_target_pairs={{0,12},{1,13},{2,14},{3,15},{4,0},{5,1},{6,2},{7,3},{8,4},{9,5},{1... | collective-permute-start | bytes 1105928 | tf_op jit(solution)/shard_map/ppermute | solution.py:278
  13.2 7.2 %shard_map.131 = bf16[2048,512]{1,0:T(8,128)(2,1)} custom-call(s32[1,2048]{1,0:T(1,128)} %perm_ref.1, bf16[3,2048,128]{2,1,0:T(8,128)(2,1)} %bitcast.23, bf16[2048,128]{1,0:T(8,128)(2,1)} %last_hbm.1), custom_call_target="tpu_custom_call" | custom-call | flops 4294967296 | bytes 4194304 | tf_op jit(solution)/shard_map/pallas_call | solution.py:91
  20.4 10.3 %all-to-all-start = ((bf16[128,16,512]{2,1,0:T(8,128)(2,1)}), bf16[128,16,512]{2,1,0:T(8,128)(2,1)S(1)}, u32[]{:S(2)}, u32[]{:S(2)}) async-start(bf16[128,16,512]{2,1,0:T(8,128)(2,1)} %bitcast.22), calls=%async_computation | async-start | bytes 4194304 | tf_op jit(solution)/shard_map/all_to_all | solution.py:287
  30.7 2.9 %collective-permute-start.5 = (bf16[4,15,3,8,128]{4,3,0,2,1:T(8,128)(2,1)S(1)}, bf16[4,15,3,8,128]{4,3,0,2,1:T(8,128)(2,1)S(1)}, u32[]{:S(2)}, u32[]{:S(2)}) collective-permute-start(bf16[4,15,3,8,128]{4,3,0,2,1:T(8,128)(2,1)S(1)} %constant_dynamic-update-slice_fusion.4), channel_id=1, source_target_pairs={{0,8},{1,9},{2,10},{3,11},{4,12},{5,13},{6,14},{7,15},{8,0},{9,1},... | collective-permute-start | bytes 1105928 | tf_op jit(solution)/shard_map/ppermute | solution.py:278
  33.6 1.5 %broadcast_in_dim.18 = bf16[16,15,3,8,128]{4,3,0,2,1:T(8,128)(2,1)} broadcast(bf16[]{:T(256)} %constant.74.clone.1), dimensions={} | broadcast | bytes 1474562 | tf_op jit(solution)/shard_map/broadcast_in_dim | solution.py:271
  35.1 0.0 copy-start.7
  35.1 0.0 copy-start.6
  35.1 0.0 copy-start.5
  35.1 0.8 constant_dynamic-update-slice_fusion.3
  35.9 0.0 collective-permute-done.3
  35.9 1.8 %constant_dynamic-update-slice_fusion.2 = bf16[16,15,3,8,128]{4,3,0,2,1:T(8,128)(2,1)} fusion(bf16[16,15,3,8,128]{4,3,0,2,1:T(8,128)(2,1)} %constant_dynamic-update-slice_fusion.3, bf16[4,15,3,8,128]{4,3,0,2,1:T(8,128)(2,1)} %collective-permute-done.3, s32[]{:T(128)S(6)} %select_n.50), kind=kLoop, calls=%fused_computation.12 | loop fusion | bytes 737284 | tf_op jit(solution)/shard_map/dynamic_update_slice | solution.py:280
  37.7 0.0 copy-start
  37.7 0.0 copy-start.1
  37.7 0.0 copy-start.2
  37.7 0.0 copy-start.4
  37.7 0.0 collective-permute-done.4
  37.7 0.8 constant_dynamic-update-slice_fusion.1
  38.5 25.4 %collective-permute-done.5 = bf16[4,15,3,8,128]{4,3,0,2,1:T(8,128)(2,1)S(1)} collective-permute-done((bf16[4,15,3,8,128]{4,3,0,2,1:T(8,128)(2,1)S(1)}, bf16[4,15,3,8,128]{4,3,0,2,1:T(8,128)(2,1)S(1)}, u32[]{:S(2)}, u32[]{:S(2)}) %collective-permute-start.5) | collective-permute-done | bytes 368672 | tf_op jit(solution)/shard_map/ppermute | solution.py:278
  63.9 0.8 constant_dynamic-update-slice_fusion
  64.7 1.0 collective-permute-start.6
  65.7 0.0 copy-done.7
  65.7 0.0 copy-done.6
  65.7 0.0 copy-done.5
  65.8 3.1 %collective-permute-done.6 = bf16[16,15,3,8,128]{4,3,0,2,1:T(8,128)(2,1)} collective-permute-done((bf16[16,15,3,8,128]{4,3,0,2,1:T(8,128)(2,1)}, bf16[16,15,3,8,128]{4,3,0,2,1:T(8,128)(2,1)}, u32[]{:S(2)}, u32[]{:S(2)}) %collective-permute-start.6) | collective-permute-done | bytes 1474592 | tf_op jit(solution)/shard_map/ppermute | solution.py:313
  68.9 0.0 all-to-all-done
  68.9 0.0 copy-done
  68.9 0.0 copy-done.1
  68.9 0.0 copy-done.2
  68.9 0.0 copy-done.4
  69.0 12.8 %shard_map.132 = bf16[2048,512]{1,0:T(8,128)(2,1)S(1)} custom-call(bf16[2048,512]{1,0:T(8,128)(2,1)S(1)} %bitcast.17, s32[2,2048]{1,0:T(2,128)S(1)} %copy-done, f32[1,2048]{1,0:T(1,128)S(1)} %bitcast.20, s32[2,1024]{1,0:T(2,128)S(1)} %copy-done.2, f32[1,1024]{1,0:T(1,128)S(1)} %bitcast.21, f32[32,1024]{1,0:T(8,128)S(1)} %pad.4.scale_ref, ...), custom_call_target="tpu_custom_call" | custom-call | flops 6039797760 | bytes 4194304 | tf_op jit(solution)/shard_map/pallas_call | solution.py:264
  81.8 0.0 copy-start.3
  81.8 37.2 %all_to_all.22 = bf16[128,16,512]{2,1,0:T(8,128)(2,1)S(1)} all-to-all(bf16[128,16,512]{2,1,0:T(8,128)(2,1)S(1)} %bitcast.18), channel_id=1, replica_groups=mesh['lat'=8,'lon'=16] {'lat','lon'}, dimensions={0} | all-to-all | bytes 4194304 | tf_op jit(solution)/shard_map/all_to_all | solution.py:287
  119.0 0.0 copy-done.3
  119.0 5.3 %shard_map.133 = (bf16[3,2048,128]{2,1,0:T(8,128)(2,1)}, bf16[2048,128]{1,0:T(8,128)(2,1)}) custom-call(s32[1,2048]{1,0:T(1,128)S(1)} %copy-done.3, bf16[2048,512]{1,0:T(8,128)(2,1)S(1)} %bitcast.19), custom_call_target="tpu_custom_call" | custom-call | flops 4294967296 | bytes 4194304 | tf_op jit(solution)/shard_map/pallas_call | solution.py:142
  (8 shorter events, 0.1 us)
Async XLA Ops:
  1.7 5.3 %collective-permute-start = (bf16[1,15,3,8,128]{4,3,0,2,1:T(8,128)(2,1)S(1)}, bf16[1,15,3,8,128]{4,3,0,2,1:T(8,128)(2,1)S(1)}, u32[]{:S(2)}, u32[]{:S(2)}) collective-permute-start(bf16[1,15,3,8,128]{4,3,0,2,1:T(8,128)(2,1)S(1)} %get-tuple-element.7), channel_id=1, source_target_pairs={{0,1},{1,2},{2,3},{3,0},{4,5},{5,6},{6,7},{7,4},{8,9},{9,10},{10,1... | collective-permute-start | bytes 276488 | tf_op jit(solution)/shard_map/ppermute | solution.py:278
  3.8 3.4 %collective-permute-start.1 = (bf16[1,15,3,8,128]{4,3,0,2,1:T(8,128)(2,1)S(1)}, bf16[1,15,3,8,128]{4,3,0,2,1:T(8,128)(2,1)S(1)}, u32[]{:S(2)}, u32[]{:S(2)}) collective-permute-start(bf16[1,15,3,8,128]{4,3,0,2,1:T(8,128)(2,1)S(1)} %get-tuple-element.7), channel_id=1, source_target_pairs={{0,3},{1,0},{2,1},{3,2},{4,7},{5,4},{6,5},{7,6},{8,11},{9,8},{10,9... | collective-permute-start | bytes 276488 | tf_op jit(solution)/shard_map/ppermute | solution.py:278
  5.1 5.2 %collective-permute-start.2 = (bf16[1,15,3,8,128]{4,3,0,2,1:T(8,128)(2,1)S(1)}, bf16[1,15,3,8,128]{4,3,0,2,1:T(8,128)(2,1)S(1)}, u32[]{:S(2)}, u32[]{:S(2)}) collective-permute-start(bf16[1,15,3,8,128]{4,3,0,2,1:T(8,128)(2,1)S(1)} %get-tuple-element.7), channel_id=1, source_target_pairs={{0,2},{1,3},{2,0},{3,1},{4,6},{5,7},{6,4},{7,5},{8,10},{9,11},{10,... | collective-permute-start | bytes 276488 | tf_op jit(solution)/shard_map/ppermute | solution.py:278
  10.3 25.6 %collective-permute-start.3 = (bf16[4,15,3,8,128]{4,3,0,2,1:T(8,128)(2,1)S(1)}, bf16[4,15,3,8,128]{4,3,0,2,1:T(8,128)(2,1)}, u32[]{:S(2)}, u32[]{:S(2)}) collective-permute-start(bf16[4,15,3,8,128]{4,3,0,2,1:T(8,128)(2,1)S(1)} %constant_dynamic-update-slice_fusion.4), channel_id=1, source_target_pairs={{0,4},{1,5},{2,6},{3,7},{4,8},{5,9},{6,10},{7,11},{8,12},{9,13},{1... | collective-permute-start | bytes 1105928 | tf_op jit(solution)/shard_map/ppermute | solution.py:278
  11.7 26.0 %collective-permute-start.4 = (bf16[4,15,3,8,128]{4,3,0,2,1:T(8,128)(2,1)S(1)}, bf16[4,15,3,8,128]{4,3,0,2,1:T(8,128)(2,1)S(1)}, u32[]{:S(2)}, u32[]{:S(2)}) collective-permute-start(bf16[4,15,3,8,128]{4,3,0,2,1:T(8,128)(2,1)S(1)} %constant_dynamic-update-slice_fusion.4), channel_id=1, source_target_pairs={{0,12},{1,13},{2,14},{3,15},{4,0},{5,1},{6,2},{7,3},{8,4},{9,5},{1... | collective-permute-start | bytes 1105928 | tf_op jit(solution)/shard_map/ppermute | solution.py:278
  20.4 48.5 %all-to-all-start = ((bf16[128,16,512]{2,1,0:T(8,128)(2,1)}), bf16[128,16,512]{2,1,0:T(8,128)(2,1)S(1)}, u32[]{:S(2)}, u32[]{:S(2)}) async-start(bf16[128,16,512]{2,1,0:T(8,128)(2,1)} %bitcast.22), calls=%async_computation | async-start | bytes 4194304 | tf_op jit(solution)/shard_map/all_to_all | solution.py:287
  30.7 33.2 %collective-permute-start.5 = (bf16[4,15,3,8,128]{4,3,0,2,1:T(8,128)(2,1)S(1)}, bf16[4,15,3,8,128]{4,3,0,2,1:T(8,128)(2,1)S(1)}, u32[]{:S(2)}, u32[]{:S(2)}) collective-permute-start(bf16[4,15,3,8,128]{4,3,0,2,1:T(8,128)(2,1)S(1)} %constant_dynamic-update-slice_fusion.4), channel_id=1, source_target_pairs={{0,8},{1,9},{2,10},{3,11},{4,12},{5,13},{6,14},{7,15},{8,0},{9,1},... | collective-permute-start | bytes 1105928 | tf_op jit(solution)/shard_map/ppermute | solution.py:278
  35.1 30.6 %copy-start.7 = (s32[1024]{0:T(1024)S(1)}, s32[1024]{0:T(1024)}, u32[]{:S(2)}) copy-start(s32[1024]{0:T(1024)} %param.21) | copy-start | bytes 12292
  35.1 30.6 %copy-start.6 = (f32[14,1024]{1,0:T(8,128)S(1)}, f32[14,1024]{1,0:T(8,128)}, u32[]{:S(2)}) copy-start(f32[14,1024]{1,0:T(8,128)} %param.20) | copy-start | bytes 172036
  35.1 30.6 %copy-start.5 = (f32[16,1024]{1,0:T(8,128)S(1)}, f32[16,1024]{1,0:T(8,128)}, u32[]{:S(2)}) copy-start(f32[16,1024]{1,0:T(8,128)} %param.19) | copy-start | bytes 196612
  37.7 31.3 %copy-start = (s32[2,2048]{1,0:T(2,128)S(1)}, s32[2,2048]{1,0:T(2,128)}, u32[]{:S(2)}) copy-start(s32[2,2048]{1,0:T(2,128)} %bidx_ref.1) | copy-start | bytes 49156
  37.7 31.3 %copy-start.1 = (f32[2048]{0:T(1024)S(1)}, f32[2048]{0:T(1024)}, u32[]{:S(2)}) copy-start(f32[2048]{0:T(1024)} %param.18) | copy-start | bytes 24580
  37.7 31.3 %copy-start.2 = (s32[2,1024]{1,0:T(2,128)S(1)}, s32[2,1024]{1,0:T(2,128)}, u32[]{:S(2)}) copy-start(s32[2,1024]{1,0:T(2,128)} %cidx_ref.1) | copy-start | bytes 24580
  37.7 31.3 %copy-start.4 = (f32[1024]{0:T(1024)S(1)}, f32[1024]{0:T(1024)}, u32[]{:S(2)}) copy-start(f32[1024]{0:T(1024)} %param.16) | copy-start | bytes 12292
  64.7 4.2 %collective-permute-start.6 = (bf16[16,15,3,8,128]{4,3,0,2,1:T(8,128)(2,1)}, bf16[16,15,3,8,128]{4,3,0,2,1:T(8,128)(2,1)}, u32[]{:S(2)}, u32[]{:S(2)}) collective-permute-start(bf16[16,15,3,8,128]{4,3,0,2,1:T(8,128)(2,1)} %constant_dynamic-update-slice_fusion), channel_id=1, source_target_pairs={{0,16},{16,0},{32,48},{48,32},{64,80},{80,64},{96,112},{112,96},{1... | collective-permute-start | bytes 4423688 | tf_op jit(solution)/shard_map/ppermute | solution.py:313
  81.8 37.2 %copy-start.3 = (s32[1,2048]{1,0:T(1,128)S(1)}, s32[1,2048]{1,0:T(1,128)}, u32[]{:S(2)}) copy-start(s32[1,2048]{1,0:T(1,128)} %perm_ref.1) | copy-start | bytes 24580
